TPU v7x, 256 devices: a whole 4x4x8 slice. The times are simulated.
256 devices in a mesh: dp: 32 (over x, z), expert: 8 (over y, core).
Axes of the slice: x: 4, y: 4, z: 8, core: 2. Of those that a mesh axis runs over, the one named last changes fastest.
Arguments:
- tokens: bfloat16 [1024, 2048], P('expert'), may hold values from -6 to 6
- cotangent: bfloat16 [1024, 2048], P('expert'), may hold values from -0.75 to 0.75
- router_logits: float32 [1024, 2], P('expert'), may hold values from -6 to 6
- routes: int32 [1024, 2], P('expert'), may hold values from 0 to 7, all different within a row; in each aligned block of 128 rows (0 to 127, 128 to 255, ...) at most 48 rows name the same one
- gate_weight: bfloat16 [8, 7168, 2048], P('expert', 'dp'), may hold values from -0.125 to 0.125
- up_weight: bfloat16 [8, 7168, 2048], P('expert', 'dp'), may hold values from -0.125 to 0.125
- down_weight: bfloat16 [8, 7168, 2048], P('expert', 'dp'), may hold values from -0.0625 to 0.0625
- dir_gate: bfloat16 [8, 7168, 2048], P('expert', 'dp'), may hold values from -0.125 to 0.125
- dir_up: bfloat16 [8, 7168, 2048], P('expert', 'dp'), may hold values from -0.125 to 0.125
- dir_down: bfloat16 [8, 7168, 2048], P('expert', 'dp'), may hold values from -0.0625 to 0.0625
Outputs:
- mixed: bfloat16 [1024, 2048], P('expert')
- hvp_gate: float32 [8, 7168, 2048], P('expert', 'dp')
- hvp_up: float32 [8, 7168, 2048], P('expert', 'dp')
- hvp_down: float32 [8, 7168, 2048], P('expert', 'dp')
Inputs may be any that keep to these rules, and one draw needn't show every extreme that they name: `routes`: each row names 2 different experts; among the 128 rows of one index of the expert axis no expert is named more than 48 times, and in every draw some block names some expert exactly 48 times.
All inputs are finite; a program needn't handle non-finite values.
Results may differ from a plain program's by a relative error of at most 0.0074.
Values may be sent and summed in bfloat16 or wider, within the bound.
A program may use at most 64 MiB of HBM per device.

v0:
```python
import jax
import jax.numpy as jnp
from jax import lax
from jax.sharding import PartitionSpec as P


def cut_along(value, dim, peers):
    before, after = (value.shape[:dim], value.shape[dim + 1 :])
    return jnp.moveaxis(value.reshape(*before, peers, -1, *after), dim, 0)


def summed_on_arrival(value, axis, dim):
    peers = lax.axis_size(axis)
    pieces = lax.all_to_all(cut_along(value, dim, peers), axis, 0, 0, tiled=True)
    return jnp.sum(pieces.astype(jnp.float32), axis=0)


def joined_along(pieces, dim):
    lengths = list(pieces.shape[1:])
    lengths[dim] *= pieces.shape[0]
    return jnp.moveaxis(pieces, 0, dim).reshape(lengths)


def sent_to_all(value, axis):
    copies = jnp.broadcast_to(value, (lax.axis_size(axis), *value.shape))
    return lax.all_to_all(copies, axis, split_axis=0, concat_axis=0, tiled=True)


def gathered_copies(value, axis, dim):
    return joined_along(sent_to_all(value, axis), dim)


def derivatives(preact):
    sigmoid_value = jax.nn.sigmoid(preact)
    slope_one = sigmoid_value * (1.0 + preact * (1.0 - sigmoid_value))
    slope_two = sigmoid_value * (1.0 - sigmoid_value) * (2.0 + preact * (1.0 - 2.0 * sigmoid_value))
    return (preact * sigmoid_value, slope_one, slope_two)


def project(left_rows, matrix):
    return jnp.einsum("rd,hd->rh", left_rows, matrix, preferred_element_type=jnp.float32)


def outer_sum(left_rows, right_rows):
    return jnp.einsum("rh,rd->hd", left_rows, right_rows, preferred_element_type=jnp.float32)


def block_terms(weights, token_rows, cot_rows):
    gate_mat, up_mat, down_mat, gate_dir, up_dir, down_dir = weights
    preact = project(token_rows, gate_mat)
    up_value = project(token_rows, up_mat)
    back_grad = project(cot_rows, down_mat)
    tang_gate = project(token_rows, gate_dir)
    tang_up = project(token_rows, up_dir)
    back_tang = project(cot_rows, down_dir)
    silu_value, slope_one, slope_two = derivatives(preact)
    hidden = (silu_value * up_value).astype(jnp.bfloat16)
    silu_tang = slope_one * tang_gate
    hidden_tang = (silu_tang * up_value + silu_value * tang_up).astype(jnp.bfloat16)
    resid_gate = (
        (back_tang * up_value + back_grad * tang_up) * slope_one
        + back_grad * up_value * slope_two * tang_gate
    ).astype(jnp.bfloat16)
    resid_up = (back_tang * silu_value + back_grad * silu_tang).astype(jnp.bfloat16)
    return (
        hidden,
        outer_sum(resid_gate, token_rows),
        outer_sum(resid_up, token_rows),
        outer_sum(hidden_tang, cot_rows),
    )


def shards(
    tokens,
    cotangent,
    router_logits,
    routes,
    gate_weight,
    up_weight,
    down_weight,
    dir_gate,
    dir_up,
    dir_down,
):
    tok_dev = tokens.shape[0]
    model_width = tokens.shape[1]
    top_count = routes.shape[1]
    experts = lax.axis_size("expert") * gate_weight.shape[0]
    capacity = top_count * tok_dev * 3 // (2 * experts)
    local_rows = experts * capacity
    weights = (gate_weight[0], up_weight[0], down_weight[0], dir_gate[0], dir_up[0], dir_down[0])
    gate_first = jax.nn.sigmoid(router_logits[:, 0] - router_logits[:, 1])
    gate_prob = jnp.stack([gate_first, 1.0 - gate_first], axis=1)
    flat_routes = routes.reshape(-1)
    onehot = (flat_routes[:, None] == jnp.arange(experts, dtype=jnp.int32)[None, :]).astype(
        jnp.int32
    )
    earlier = jnp.cumsum(onehot, axis=0) - onehot
    slot_pos = jnp.sum(earlier * onehot, axis=1)
    slot_index = flat_routes * capacity + slot_pos
    dispatch = (jnp.arange(local_rows, dtype=jnp.int32)[:, None] == slot_index[None, :]).astype(
        jnp.bfloat16
    )
    repeated = jnp.repeat(tokens, top_count, axis=0)
    scaled = (
        gate_prob.reshape(-1)[:, None]
        * jnp.repeat(cotangent, top_count, axis=0).astype(jnp.float32)
    ).astype(jnp.bfloat16)
    send_rows = (
        jnp.dot(dispatch, repeated, preferred_element_type=jnp.float32)
        .astype(jnp.bfloat16)
        .reshape(experts, capacity, model_width)
    )
    send_cot = (
        jnp.dot(dispatch, scaled, preferred_element_type=jnp.float32)
        .astype(jnp.bfloat16)
        .reshape(experts, capacity, model_width)
    )
    arrived_rows, arrived_cot = (
        lax.all_to_all(send_rows, "expert", split_axis=0, concat_axis=0, tiled=True),
        lax.all_to_all(send_cot, "expert", split_axis=0, concat_axis=0, tiled=True),
    )
    hidden, hvp_gate, hvp_up, hvp_down = block_terms(
        weights,
        arrived_rows.reshape(local_rows, model_width),
        arrived_cot.reshape(local_rows, model_width),
    )
    partial_out = jnp.dot(hidden, weights[2], preferred_element_type=jnp.float32)
    shares = summed_on_arrival(partial_out.astype(jnp.bfloat16), "dp", 1)
    share_width = shares.shape[1]
    expert_out = shares.astype(jnp.bfloat16).reshape(experts, capacity, share_width)
    returned = lax.all_to_all(expert_out, "expert", split_axis=0, concat_axis=0, tiled=True)
    picked = jnp.dot(
        dispatch.T, returned.reshape(local_rows, share_width), preferred_element_type=jnp.float32
    ).reshape(tok_dev, top_count, share_width)
    mixed_share = jnp.sum(gate_prob[:, :, None] * picked, axis=1).astype(jnp.bfloat16)
    mixed = gathered_copies(mixed_share, "dp", 1)
    return (mixed, hvp_gate[None], hvp_up[None], hvp_down[None])


def solution(mesh):
    in_specs = (
        P("expert", None),
        P("expert", None),
        P("expert", None),
        P("expert", None),
        P("expert", "dp", None),
        P("expert", "dp", None),
        P("expert", "dp", None),
        P("expert", "dp", None),
        P("expert", "dp", None),
        P("expert", "dp", None),
    )
    out_specs = (
        P("expert", None),
        P("expert", "dp", None),
        P("expert", "dp", None),
        P("expert", "dp", None),
    )
    return jax.shard_map(shards, mesh=mesh, in_specs=in_specs, out_specs=out_specs, check_vma=False)
```

profile of v0, /device:TPU:32, one launch (start us, length us, event | category | flops | bytes accessed | tf_op | source)
XLA Modules:
  0.0 152.5 jit_solution(13120432840209204215)
XLA Ops:
  2.8 1.7 %broadcast_in_dim.22 = bf16[128,2,2048]{2,1,0:T(2,128)(2,1)S(1)} broadcast(bf16[128,2048]{1,0:T(8,128)(2,1)} %param.10), dimensions={0,2} | broadcast | bytes 1572864 | tf_op jit(solution)/shard_map/broadcast_in_dim | solution.py:104
  5.5 26.0 %all_to_all.25 = bf16[8,48,2048]{2,1,0:T(8,128)(2,1)S(1)} all-to-all(bf16[8,48,2048]{2,1,0:T(8,128)(2,1)S(1)} %bitcast.68), channel_id=1, replica_groups=mesh['dp'=32,'expert'=8] {'expert'}, dimensions={0} | all-to-all | bytes 3145728 | tf_op jit(solution)/shard_map/all_to_all | solution.py:120
  33.4 1.8 %convolution_convert_fusion.1 = bf16[384,2048]{1,0:T(8,128)(2,1)} fusion(bf16[1,224,2048]{2,1,0:T(8,128)(2,1)S(1)} %copy-done, f32[384,224]{0,1:T(8,128)S(1)} %fusion.11, f32[384,224]{0,1:T(8,128)S(1)} %fusion.13), kind=kOutput, calls=%fused_computation.1 | convolution fusion | flops 353624064 | bytes 3178496 | tf_op jit(solution)/shard_map/dot_general | solution.py:128
  35.1 2.6 %copy.22 = bf16[384,2048]{0,1:T(8,128)(2,1)} copy(bf16[384,2048]{1,0:T(8,128)(2,1)} %convolution_convert_fusion.1) | data formatting | bytes 3145728 | tf_op jit(solution)/shard_map/convert_element_type | solution.py:129
  37.7 11.4 %all-to-all-start.1 = ((bf16[32,384,64]{1,2,0:T(8,128)(2,1)}), bf16[32,384,64]{1,2,0:T(8,128)(2,1)}, u32[]{:S(2)}, u32[]{:S(2)}) async-start(bf16[32,384,64]{1,2,0:T(8,128)(2,1)} %bitcast.67), calls=%async_computation.1 | async-start | bytes 3145728 | tf_op jit(solution)/shard_map/all_to_all | solution.py:14
  49.4 3.5 %broadcast_in_dim.24 = f32[128,2,2048]{2,1,0:T(2,128)} broadcast(bf16[128,2048]{1,0:T(8,128)(2,1)} %param.11), dimensions={0,2} | broadcast | bytes 2621440 | tf_op jit(solution)/shard_map/broadcast_in_dim | solution.py:107
  52.8 3.7 %convert_element_type.51 = f32[256,2048]{1,0:T(8,128)} reshape(f32[128,2,2048]{2,1,0:T(2,128)} %broadcast_in_dim.24) | data formatting | bytes 4194304 | tf_op jit(solution)/shard_map/convert_element_type | solution.py:107
  56.5 3.4 %convolution_convert_fusion = bf16[384,2048]{1,0:T(8,128)(2,1)} fusion(f32[256,2048]{1,0:T(8,128)} %convert_element_type.51, f32[256]{0:T(256)S(1)} %mul.95, s32[256]{0:T(256)S(1)} %multiply_add_fusion), kind=kOutput, calls=%fused_computation | convolution fusion | flops 404586496 | bytes 3672064 | tf_op jit(solution)/shard_map/dot_general | solution.py:115
  59.9 28.3 %all-to-all-done.1 = bf16[32,384,64]{1,2,0:T(8,128)(2,1)} async-done(((bf16[32,384,64]{1,2,0:T(8,128)(2,1)}), bf16[32,384,64]{1,2,0:T(8,128)(2,1)}, u32[]{:S(2)}, u32[]{:S(2)}) %all-to-all-start.1) | async-done | bytes 1572896 | tf_op jit(solution)/shard_map/all_to_all | solution.py:14
  88.2 4.3 %all-to-all-start.4 = ((bf16[8,48,2048]{2,1,0:T(8,128)(2,1)}), bf16[8,48,2048]{2,1,0:T(8,128)(2,1)}, u32[]{:S(2)}, u32[]{:S(2)}) async-start(bf16[8,48,2048]{2,1,0:T(8,128)(2,1)} %bitcast.66), calls=%async_computation.4 | async-start | bytes 3145728 | tf_op jit(solution)/shard_map/all_to_all | solution.py:121
  93.5 2.0 %fusion.2 = f32[384,224]{0,1:T(8,128)S(1)} fusion(bf16[384,2048]{1,0:T(8,128)(2,1)S(1)} %bitcast.62, bf16[1,224,2048]{2,1,0:T(8,128)(2,1)} %param.17), kind=kOutput, calls=%fused_computation.10 | convolution fusion | flops 352321536 | bytes 2834432 | tf_op jit(solution)/shard_map/rd,hd->rh/dot_general | solution.py:41
  96.9 2.3 %reduce_sum.31 = bf16[384,64]{0,1:T(8,128)(2,1)} reduce(bf16[32,384,64]{1,2,0:T(8,128)(2,1)} %all-to-all-done.1, bf16[]{:T(256)} %constant.14.clone.1), dimensions={0}, to_apply=%region_3.4 | reduce | flops 761856 | bytes 1622018 | tf_op jit(solution)/shard_map/reduce_sum | solution.py:15
  100.7 1.6 %reshape.106 = bf16[8,2,1536]{2,1,0:T(2,128)(2,1)} reshape(bf16[8,48,64]{2,1,0:T(8,128)(2,1)} %bitcast.69) | data formatting | bytes 98304
  102.3 11.8 %all-to-all-done.4 = bf16[8,48,2048]{2,1,0:T(8,128)(2,1)} async-done(((bf16[8,48,2048]{2,1,0:T(8,128)(2,1)}), bf16[8,48,2048]{2,1,0:T(8,128)(2,1)}, u32[]{:S(2)}, u32[]{:S(2)}) %all-to-all-start.4) | async-done | bytes 1572896 | tf_op jit(solution)/shard_map/all_to_all | solution.py:121
  114.1 4.0 %all-to-all-start.2 = ((bf16[8,2,1536]{2,1,0:T(2,128)(2,1)}), bf16[8,2,1536]{2,1,0:T(2,128)(2,1)}, u32[]{:S(2)}, u32[]{:S(2)}) async-start(bf16[8,2,1536]{2,1,0:T(2,128)(2,1)} %reshape.106), calls=%async_computation.2 | async-start | bytes 98304 | tf_op jit(solution)/shard_map/all_to_all | solution.py:132
  118.1 2.8 %fusion.8 = f32[384,224]{0,1:T(8,128)} fusion(bf16[384,2048]{1,0:T(8,128)(2,1)} %bitcast.15, bf16[1,224,2048]{2,1,0:T(8,128)(2,1)S(1)} %copy-done), kind=kOutput, calls=%fused_computation.16 | convolution fusion | flops 352321536 | bytes 2834432 | tf_op jit(solution)/shard_map/rd,hd->rh/dot_general | solution.py:41
  120.9 2.7 %all-to-all-done.2 = bf16[8,2,1536]{2,1,0:T(2,128)(2,1)} async-done(((bf16[8,2,1536]{2,1,0:T(2,128)(2,1)}), bf16[8,2,1536]{2,1,0:T(2,128)(2,1)}, u32[]{:S(2)}, u32[]{:S(2)}) %all-to-all-start.2) | async-done | bytes 49184 | tf_op jit(solution)/shard_map/all_to_all | solution.py:132
  127.3 5.6 %all-to-all-start.3 = ((bf16[32,128,64]{1,2,0:T(8,128)(2,1)}), bf16[32,128,64]{1,2,0:T(8,128)(2,1)}, u32[]{:S(2)}, u32[]{:S(2)}) async-start(bf16[32,128,64]{1,2,0:T(8,128)(2,1)} %broadcast_in_dim.23), calls=%async_computation.3 | async-start | bytes 1048576 | tf_op jit(solution)/shard_map/all_to_all | solution.py:26
  132.9 3.6 %convolution_bitcast_fusion = f32[1,224,2048]{2,1,0:T(8,128)} fusion(bf16[384,2048]{1,0:T(8,128)(2,1)} %bitcast.15, f32[384,224]{0,1:T(8,128)} %fusion.4, f32[384,224]{0,1:T(8,128)S(1)} %fusion.11, f32[384,224]{0,1:T(8,128)S(1)} %fusion.2, f32[384,224]{0,1:T(8,128)S(1)} %fusion.13), kind=kOutput, calls=%fused_computation.3 | convolution fusion | flops 353439744 | bytes 4784128 | tf_op jit(solution)/shard_map/rh,rd->hd/dot_general | solution.py:45
  136.4 2.2 %fusion.6 = f32[384,224]{0,1:T(8,128)S(1)} fusion(bf16[384,2048]{1,0:T(8,128)(2,1)} %bitcast.15, bf16[1,224,2048]{2,1,0:T(8,128)(2,1)S(1)} %copy-done.6), kind=kOutput, calls=%fused_computation.14 | convolution fusion | flops 352321536 | bytes 2834432 | tf_op jit(solution)/shard_map/rd,hd->rh/dot_general | solution.py:41
  138.6 1.9 %convolution_bitcast_fusion.1 = f32[1,224,2048]{2,1,0:T(8,128)} fusion(bf16[384,2048]{1,0:T(8,128)(2,1)S(1)} %bitcast.64, f32[384,224]{0,1:T(8,128)S(1)} %copy-done.2, f32[384,224]{0,1:T(8,128)S(1)} %fusion.6, f32[384,224]{0,1:T(8,128)S(1)} %fusion.2, f32[384,224]{0,1:T(8,128)S(1)} %fusion.13), kind=kOutput, calls=%fused_computation.4 | convolution fusion | flops 353439744 | bytes 4784128 | tf_op jit(solution)/shard_map/rh,rd->hd/dot_general | solution.py:45
  140.6 2.0 %convolution_bitcast_fusion.2 = f32[1,224,2048]{2,1,0:T(8,128)} fusion(bf16[384,2048]{1,0:T(8,128)(2,1)S(1)} %bitcast.65, f32[384,224]{0,1:T(8,128)S(1)} %fusion.2, f32[384,224]{0,1:T(8,128)S(1)} %fusion.13, f32[384,224]{0,1:T(8,128)S(1)} %copy-done.2, f32[384,224]{0,1:T(8,128)S(1)} %fusion.11, f32[384,224]{0,1:T(8,128)S(1)} %copy-done.1, ...), kind=kOutput, calls=%fused_computation.5 | convolution fusion | flops 354213888 | bytes 5472256 | tf_op jit(solution)/shard_map/rh,rd->hd/dot_general | solution.py:45
  142.6 7.9 %all-to-all-done.3 = bf16[32,128,64]{1,2,0:T(8,128)(2,1)} async-done(((bf16[32,128,64]{1,2,0:T(8,128)(2,1)}), bf16[32,128,64]{1,2,0:T(8,128)(2,1)}, u32[]{:S(2)}, u32[]{:S(2)}) %all-to-all-start.3) | async-done | bytes 524320 | tf_op jit(solution)/shard_map/all_to_all | solution.py:26
  150.4 2.0 %copy.27 = bf16[128,2048]{1,0:T(8,128)(2,1)} copy(bf16[128,2048]{0,1:T(8,128)(2,1)} %bitcast.13) | data formatting | bytes 1048576
  (41 shorter events, 12.9 us)
Async XLA Ops:
  0.6 32.7 %copy-start = (bf16[1,224,2048]{2,1,0:T(8,128)(2,1)S(1)}, bf16[1,224,2048]{2,1,0:T(8,128)(2,1)}, u32[]{:S(2)}) copy-start(bf16[1,224,2048]{2,1,0:T(8,128)(2,1)} %param.16) | copy-start | bytes 2752516
  5.5 26.0 %copy-start.3 = (bf16[1,224,2048]{2,1,0:T(8,128)(2,1)S(1)}, bf16[1,224,2048]{2,1,0:T(8,128)(2,1)}, u32[]{:S(2)}) copy-start(bf16[1,224,2048]{2,1,0:T(8,128)(2,1)} %param.14) | copy-start | bytes 2752516
  31.5 1.2 copy-start.4
  37.7 11.4 %copy-start.7 = (f32[128,2]{0,1:T(2,128)S(1)}, f32[128,2]{0,1:T(2,128)}, u32[]{:S(2)}) copy-start(f32[128,2]{0,1:T(2,128)} %param.12) | copy-start | bytes 3076
  37.7 50.5 %all-to-all-start.1 = ((bf16[32,384,64]{1,2,0:T(8,128)(2,1)}), bf16[32,384,64]{1,2,0:T(8,128)(2,1)}, u32[]{:S(2)}, u32[]{:S(2)}) async-start(bf16[32,384,64]{1,2,0:T(8,128)(2,1)} %bitcast.67), calls=%async_computation.1 | async-start | bytes 3145728 | tf_op jit(solution)/shard_map/all_to_all | solution.py:14
  88.2 25.9 %all-to-all-start.4 = ((bf16[8,48,2048]{2,1,0:T(8,128)(2,1)}), bf16[8,48,2048]{2,1,0:T(8,128)(2,1)}, u32[]{:S(2)}, u32[]{:S(2)}) async-start(bf16[8,48,2048]{2,1,0:T(8,128)(2,1)} %bitcast.66), calls=%async_computation.4 | async-start | bytes 3145728 | tf_op jit(solution)/shard_map/all_to_all | solution.py:121
  93.4 2.0 %copy-start.5 = (bf16[1,224,2048]{2,1,0:T(8,128)(2,1)S(1)}, bf16[1,224,2048]{2,1,0:T(8,128)(2,1)}, u32[]{:S(2)}) copy-start(bf16[1,224,2048]{2,1,0:T(8,128)(2,1)} %param.18) | copy-start | bytes 2752516
  114.1 9.5 %all-to-all-start.2 = ((bf16[8,2,1536]{2,1,0:T(2,128)(2,1)}), bf16[8,2,1536]{2,1,0:T(2,128)(2,1)}, u32[]{:S(2)}, u32[]{:S(2)}) async-start(bf16[8,2,1536]{2,1,0:T(2,128)(2,1)} %reshape.106), calls=%async_computation.2 | async-start | bytes 98304 | tf_op jit(solution)/shard_map/all_to_all | solution.py:132
  127.3 23.1 %all-to-all-start.3 = ((bf16[32,128,64]{1,2,0:T(8,128)(2,1)}), bf16[32,128,64]{1,2,0:T(8,128)(2,1)}, u32[]{:S(2)}, u32[]{:S(2)}) async-start(bf16[32,128,64]{1,2,0:T(8,128)(2,1)} %broadcast_in_dim.23), calls=%async_computation.3 | async-start | bytes 1048576 | tf_op jit(solution)/shard_map/all_to_all | solution.py:26
  132.9 3.6 %copy-start.6 = (bf16[1,224,2048]{2,1,0:T(8,128)(2,1)S(1)}, bf16[1,224,2048]{2,1,0:T(8,128)(2,1)}, u32[]{:S(2)}) copy-start(bf16[1,224,2048]{2,1,0:T(8,128)(2,1)} %param.19) | copy-start | bytes 2752516
  136.4 2.2 %copy-start.2 = (f32[384,224]{0,1:T(8,128)S(1)}, f32[384,224]{0,1:T(8,128)}, u32[]{:S(2)}) copy-start(f32[384,224]{0,1:T(8,128)} %fusion.8) | copy-start | bytes 1032196
  138.6 2.0 %copy-start.1 = (f32[384,224]{0,1:T(8,128)S(1)}, f32[384,224]{0,1:T(8,128)}, u32[]{:S(2)}) copy-start(f32[384,224]{0,1:T(8,128)} %fusion.4) | copy-start | bytes 1032196
where the time goes:
time: 154 us; the launch traced here: 152 us
  waiting for transfers between devices  50.7 us (33%)
  blocking collectives  26 us (17%)
  starting transfers between devices  25.2 us (16%)
  matrix products  24.2 us (16%)
  local copies, waits for them, and re-layouts  22.4 us (15%)
  other arithmetic  3.12 us (2%)
    all_to_all x1, waiting for transfers between devices, summed_on_arrival(): lax.all_to_all(cut_along(value, dim, peers), axis, 0, 0, tiled=True)  28.3 us
    all_to_all x1, blocking collectives, shards(): lax.all_to_all(send_rows, 'expert', split_axis=0, concat_axis=0, tiled=True)  26 us
    all_to_all x1, waiting for transfers between devices, shards(): lax.all_to_all(send_cot, 'expert', split_axis=0, concat_axis=0, tiled=True)  11.8 us
    all_to_all x1, starting transfers between devices, summed_on_arrival(): lax.all_to_all(cut_along(value, dim, peers), axis, 0, 0, tiled=True)  11.4 us
    dot_general x6, matrix products, project(): jnp.einsum('rd,hd->rh', left_rows, matrix, preferred_element_type=jnp.flo...  9.79 us
    all_to_all x1, waiting for transfers between devices, sent_to_all(): return lax.all_to_all(copies, axis, split_axis=0, concat_axis=0, tiled=True)  7.85 us
    dot_general x3, matrix products, outer_sum(): jnp.einsum('rh,rd->hd', left_rows, right_rows, preferred_element_type=jnp...  7.52 us
    unnamed x20, local copies, waits for them, and re-layouts  6.61 us
  transfers between devices with their start and end apart: 4, of which 4 were waited for; matrix products, arithmetic and copies ran while one was open for 22% of the time, Pallas kernels for 0%

commit v1 on v0

v1 whole, which is shorter than its diff:
```python
import functools

import jax
import jax.numpy as jnp
from jax import lax
from jax.experimental import pallas as pl
from jax.experimental.pallas import tpu as pltpu
from jax.sharding import PartitionSpec as P

MESH = pl.DeviceIdType.MESH
F32 = jnp.float32
BF16 = jnp.bfloat16
NZ = 8
NC = 2
LANES = 128


def dot_nt(left, right):
    return lax.dot_general(left, right, (((1,), (1,)), ((), ())), preferred_element_type=F32)


def dot_tn(left, right):
    return lax.dot_general(left, right, (((0,), (0,)), ((), ())), preferred_element_type=F32)


def dot_nn(left, right):
    return jnp.dot(left, right, preferred_element_type=F32)


def aligned(index, size):
    return pl.multiple_of(index * size, size)


def layer_kernel(nx, ny, cap, *refs):
    (
        tok_hbm, cot_hbm, logits_ref, routes_ref, g_hbm, u_hbm, w_hbm, vg_hbm, vu_hbm, vw_hbm,
        mixed_hbm, slotx_hbm, slotc_hbm, resid_hbm,
        tok, cot, g, u, w, vg, vu, vw,
        disp, prob_t, send_x, send_c, slot_x, slot_c,
        xsend, xrecv, xown, zsend, zrecv, ret_send, ret, mixed, resid,
        load_sem, tok_ss, tok_rs, cot_ss, cot_rs, x_ss, x_rs, z_ss, z_rs, r_ss, r_rs,
        gz_ss, gz_rs, gx_ss, gx_rs, out_sem,
    ) = refs
    tokens, width = tok.shape
    xw = width // nx
    pair = NC * cap
    rows = ny * pair

    dp = lax.axis_index("dp")
    e = lax.axis_index("expert")
    x, z = dp // NZ, dp % NZ
    y, c = e // NC, e % NC
    parity = z % NC
    away = (c + parity) % NC

    def device(dx=0, dz=0, dy=0, dc=0):
        return (((x + dx) % nx) * NZ + (z + dz) % NZ, ((y + dy) % ny) * NC + (c + dc) % NC)

    loads = []
    for number, (src, dst) in enumerate(
        [(tok_hbm, tok), (cot_hbm, cot), (g_hbm, g), (u_hbm, u), (w_hbm, w), (vg_hbm, vg), (vu_hbm, vu), (vw_hbm, vw)]
    ):
        copy = pltpu.make_async_copy(src, dst, load_sem.at[number])
        copy.start()
        loads.append(copy)

    barrier = pltpu.get_barrier_semaphore()
    peers = []
    for dx in range(1, nx):
        peers.append(dict(dx=dx))
    for dz in range(1, NZ):
        peers.append(dict(dz=dz))
    for dy in range(ny):
        for dc in range(NC):
            if dy or dc:
                peers.append(dict(dy=dy, dc=dc))
    for peer in peers:
        pl.semaphore_signal(barrier, inc=1, device_id=device(**peer), device_id_type=MESH)

    experts = ny * NC
    expert_iota = lax.broadcasted_iota(jnp.int32, (experts, tokens), 0)
    route0, route1 = routes_ref[0:1, :], routes_ref[1:2, :]
    hot0 = (expert_iota == route0).astype(F32)
    hot1 = (expert_iota == route1).astype(F32)
    before = (
        lax.broadcasted_iota(jnp.int32, (tokens, tokens), 0)
        < lax.broadcasted_iota(jnp.int32, (tokens, tokens), 1)
    ).astype(BF16)
    earlier = dot_nn((hot0 + hot1).astype(BF16), before)
    pos0 = jnp.sum(earlier * hot0, axis=0, keepdims=True).astype(jnp.int32)
    pos1 = jnp.sum(earlier * hot1, axis=0, keepdims=True).astype(jnp.int32)
    slot_iota = lax.broadcasted_iota(jnp.int32, (rows, tokens), 0)
    disp[:, :tokens] = (slot_iota == route0 * cap + pos0).astype(F32).astype(BF16)
    disp[:, tokens:] = (slot_iota == route1 * cap + pos1).astype(F32).astype(BF16)
    first = jax.nn.sigmoid(logits_ref[0:1, :] - logits_ref[1:2, :])
    prob_t[0] = jnp.transpose(jnp.broadcast_to(first, (LANES, tokens)))
    prob_t[1] = 1.0 - prob_t[0]

    pl.semaphore_wait(barrier, len(peers))

    sends = []

    def send(src, dst, ss, rs, target):
        copy = pltpu.make_async_remote_copy(
            src_ref=src, dst_ref=dst, send_sem=ss, recv_sem=rs, device_id=target, device_id_type=MESH
        )
        copy.start()
        sends.append(copy)
        return copy

    my_rows = pl.ds(aligned(e, cap), cap)
    order = [dy for dy in (1, ny - 1, 2) if dy < ny]
    order = [dy for i, dy in enumerate(order) if dy not in order[:i]] + [0]

    def dispatch(buffer, target_buffer, ss, rs, values, hot):
        copies = {}
        for dy in order:
            yy = (y + dy) % ny
            block = pl.ds(aligned(yy, pair), pair)
            buffer[block, :] = dot_nn(hot(block), values).astype(BF16)
            for dc in range(NC):
                if dy == 0 and dc == 0:
                    target_buffer[my_rows, :] = buffer[my_rows, :]
                    continue
                ee = yy * NC + (c + dc) % NC
                number = dy * NC + dc
                copies[number] = send(
                    buffer.at[pl.ds(aligned(ee, cap), cap)], target_buffer.at[my_rows],
                    ss.at[number], rs.at[number], device(dy=dy, dc=dc),
                )
        return copies

    loads[0].wait()
    tok_copies = dispatch(
        send_x, slot_x, tok_ss, tok_rs, tok[...],
        lambda block: disp[block, :tokens] + disp[block, tokens:],
    )
    loads[1].wait()
    cot_f = cot[...].astype(F32)
    scaled = jnp.concatenate(
        [(prob_t[0][:, 0:1] * cot_f).astype(BF16), (prob_t[1][:, 0:1] * cot_f).astype(BF16)], axis=0
    )
    cot_copies = dispatch(send_c, slot_c, cot_ss, cot_rs, scaled, lambda block: disp[block, :])

    for copy in loads[2:5]:
        copy.wait()

    def group_rows(dy):
        return pl.ds(aligned((y - dy) % ny, pair), pair)

    x_copies, z_copies = {}, {}

    def forward(dy):
        for dc in range(NC):
            if dy or dc:
                tok_copies[dy * NC + dc].wait_recv()
        rows_x = slot_x[group_rows(dy), :]
        pre = dot_nt(rows_x, g[...])
        up = dot_nt(rows_x, u[...])
        hidden = (pre * jax.nn.sigmoid(pre) * up).astype(BF16)
        for dx in list(range(1, nx)) + [0]:
            xx = (x + dx) % nx
            part = dot_nn(hidden, w[:, pl.ds(aligned(xx, xw), xw)])
            if dx == 0:
                xown[dy] = part
            else:
                xsend[dy, dx - 1] = part.astype(BF16)
                x_copies[dy, dx] = send(
                    xsend.at[dy, dx - 1], xrecv.at[dy, dx - 1],
                    x_ss.at[dy, dx - 1], x_rs.at[dy, dx - 1], device(dx=dx),
                )

    def reduce_x(dy):
        total = xown[dy]
        for dx in range(1, nx):
            x_copies[dy, dx].wait_recv()
            total = total + xrecv[dy, dx - 1].astype(F32)
        zsend[dy] = total.astype(BF16)
        for dz in (4, 3, 5, 2, 6, 1, 7):
            if dz >= NZ:
                continue
            zz = (z + dz) % NZ
            src = zsend.at[dy, pl.ds(aligned(zz % NC, cap), cap), pl.ds(aligned(zz // NC, LANES), LANES)]
            z_copies[dy, dz] = send(
                src, zrecv.at[dy, dz - 1], z_ss.at[dy, dz - 1], z_rs.at[dy, dz - 1], device(dz=dz)
            )

    def reduce_z(dy):
        total = zsend[dy, pl.ds(aligned(parity, cap), cap), pl.ds(aligned(z // NC, LANES), LANES)].astype(F32)
        for dz in range(1, NZ):
            z_copies[dy, dz].wait_recv()
            total = total + zrecv[dy, dz - 1].astype(F32)
        if dy == 0:
            @pl.when(away == 0)
            def _():
                ret[my_rows, :] = total.astype(BF16)

            @pl.when(away == 1)
            def _():
                ret_send[dy] = total.astype(BF16)
                ret_copy(dy).start()
        else:
            ret_send[dy] = total.astype(BF16)
            ret_copy(dy).start()

    def ret_copy(dy):
        return pltpu.make_async_remote_copy(
            src_ref=ret_send.at[dy], dst_ref=ret.at[my_rows], send_sem=r_ss.at[dy],
            recv_sem=r_rs.at[dy * NC + away],
            device_id=(dp, ((y - dy) % ny) * NC + parity), device_id_type=MESH,
        )

    groups = [0] + [dy for dy in order if dy]
    for position, dy in enumerate(groups):
        forward(dy)
        if position >= 2:
            reduce_x(groups[position - 2])
    reduce_x(groups[-2])
    for dy in groups[:-2]:
        reduce_z(dy)
    reduce_x(groups[-1])

    for copy in loads[5:8]:
        copy.wait()
    all_x = slot_x[...]
    pre = dot_nt(g[...], all_x)
    up = dot_nt(u[...], all_x)
    tang_gate = dot_nt(vg[...], all_x)
    tang_up = dot_nt(vu[...], all_x)
    copy_x = pltpu.make_async_copy(slot_x, slotx_hbm, out_sem.at[0])
    copy_x.start()

    reduce_z(groups[-2])
    reduce_z(groups[-1])

    def piece(xx, zz):
        return mixed.at[:, pl.ds(aligned(xx * (xw // LANES) + zz // NC, LANES), LANES)]

    def gather_z(dz):
        return pltpu.make_async_remote_copy(
            src_ref=piece(x, z), dst_ref=piece(x, z), send_sem=gz_ss.at[dz - 1],
            recv_sem=gz_rs.at[dz - 1], device_id=device(dz=dz), device_id_type=MESH,
        )

    @pl.when(away == 0)
    def _():
        for dy in range(ny):
            for dc in range(NC):
                if dy or dc:
                    pltpu.make_async_remote_copy(
                        src_ref=ret_send.at[dy], dst_ref=ret.at[pl.ds(aligned(((y + dy) % ny) * NC + (c + dc) % NC, cap), cap)],
                        send_sem=r_ss.at[dy], recv_sem=r_rs.at[dy * NC + dc],
                        device_id=(dp, e), device_id_type=MESH,
                    ).wait_recv()
        returned = ret[...]
        picked0 = dot_tn(disp[:, :tokens], returned)
        picked1 = dot_tn(disp[:, tokens:], returned)
        piece(x, z)[...] = (prob_t[0] * picked0 + prob_t[1] * picked1).astype(BF16)
        for dz in range(1, NZ):
            gather_z(dz).start()

    x_gathers = []
    for number in (0, 1, NZ // NC - 1, 2):
        if number >= NZ // NC or number in [n for n, _ in x_gathers]:
            continue
        back = NC * number + away
        zz = (z + NZ - back) % NZ

        def arrived(dz):
            pltpu.make_async_remote_copy(
                src_ref=piece(x, zz), dst_ref=piece(x, zz), send_sem=gz_ss.at[dz - 1],
                recv_sem=gz_rs.at[dz - 1], device_id=(dp, e), device_id_type=MESH,
            ).wait_recv()

        if number == 0:
            @pl.when(away == 1)
            def _():
                arrived(1)
        else:
            arrived(NC * number + away)
        for dx in range(1, nx):
            copy = pltpu.make_async_remote_copy(
                src_ref=piece(x, zz), dst_ref=piece(x, zz), send_sem=gx_ss.at[number, dx - 1],
                recv_sem=gx_rs.at[number, dx - 1], device_id=device(dx=dx), device_id_type=MESH,
            )
            copy.start()
            x_gathers.append((number, copy))

    for copy in cot_copies.values():
        copy.wait_recv()
    copy_c = pltpu.make_async_copy(slot_c, slotc_hbm, out_sem.at[1])
    copy_c.start()
    all_c = slot_c[...]
    back_grad = dot_nt(w[...], all_c)
    back_tang = dot_nt(vw[...], all_c)
    sig = jax.nn.sigmoid(pre)
    silu = pre * sig
    slope_one = sig * (1.0 + pre * (1.0 - sig))
    slope_two = sig * (1.0 - sig) * (2.0 + pre * (1.0 - 2.0 * sig))
    silu_tang = slope_one * tang_gate
    resid[2] = (silu_tang * up + silu * tang_up).astype(BF16)
    resid[0] = (
        (back_tang * up + back_grad * tang_up) * slope_one + back_grad * up * slope_two * tang_gate
    ).astype(BF16)
    resid[1] = (back_tang * silu + back_grad * silu_tang).astype(BF16)
    copy_r = pltpu.make_async_copy(resid, resid_hbm, out_sem.at[2])
    copy_r.start()

    for _, copy in x_gathers:
        copy.wait_recv()
    copy_m = pltpu.make_async_copy(mixed, mixed_hbm, out_sem.at[3])
    copy_m.start()

    for copy in sends:
        copy.wait_send()
    for _, copy in x_gathers:
        copy.wait_send()
    for dy in range(1, ny):
        ret_copy(dy).wait_send()

    @pl.when(away == 1)
    def _():
        ret_copy(0).wait_send()

    @pl.when(away == 0)
    def _():
        for dz in range(1, NZ):
            gather_z(dz).wait_send()

    copy_x.wait()
    copy_c.wait()
    copy_r.wait()
    copy_m.wait()


def outer_kernel(resid, slot_x, slot_c, gate, up, down):
    rows_x = slot_x[...]
    gate[...] = dot_nn(resid[0], rows_x)
    up[...] = dot_nn(resid[1], rows_x)
    down[...] = dot_nn(resid[2], slot_c[...])


def outer_sums(resid, slot_x, slot_c):
    _, hidden, rows = resid.shape
    width = slot_x.shape[1]
    step = width // 4
    out = jax.ShapeDtypeStruct((hidden, width), F32)
    column = lambda i: (0, i)
    return pl.pallas_call(
        outer_kernel,
        grid=(width // step,),
        out_shape=(out, out, out),
        in_specs=[
            pl.BlockSpec((3, hidden, rows), lambda i: (0, 0, 0)),
            pl.BlockSpec((rows, step), column),
            pl.BlockSpec((rows, step), column),
        ],
        out_specs=[pl.BlockSpec((hidden, step), column)] * 3,
    )(resid, slot_x, slot_c)


def shards(nx, ny, tokens, cotangent, router_logits, routes, *weights):
    count, width = tokens.shape
    hidden = weights[0].shape[1]
    cap = routes.shape[1] * count * 3 // (2 * ny * NC)
    pair = NC * cap
    rows = ny * pair
    xw = width // nx
    weights = [each.reshape(hidden, width) for each in weights]
    dma = pltpu.SemaphoreType.DMA
    vmem = pltpu.VMEM
    any_spec = pl.BlockSpec(memory_space=pl.ANY)
    vmem_spec = pl.BlockSpec(memory_space=pltpu.VMEM)
    sds = jax.ShapeDtypeStruct
    mixed, slot_x, slot_c, resid = pl.pallas_call(
        functools.partial(layer_kernel, nx, ny, cap),
        out_shape=(
            sds((count, width), BF16), sds((rows, width), BF16), sds((rows, width), BF16),
            sds((3, hidden, rows), BF16),
        ),
        in_specs=[any_spec, any_spec, vmem_spec, vmem_spec] + [any_spec] * 6,
        out_specs=[any_spec] * 4,
        scratch_shapes=[vmem((count, width), BF16)] * 2
        + [vmem((hidden, width), BF16)] * 6
        + [vmem((rows, 2 * count), BF16), vmem((2, count, LANES), F32)]
        + [vmem((rows, width), BF16)] * 4
        + [
            vmem((ny, nx - 1, pair, xw), BF16), vmem((ny, nx - 1, pair, xw), BF16),
            vmem((ny, pair, xw), F32), vmem((ny, pair, xw), BF16),
            vmem((ny, NZ - 1, cap, LANES), BF16), vmem((ny, cap, LANES), BF16),
            vmem((rows, LANES), BF16), vmem((count, width), BF16), vmem((3, hidden, rows), BF16),
            dma((8,)), dma((ny * NC,)), dma((ny * NC,)), dma((ny * NC,)), dma((ny * NC,)),
            dma((ny, nx - 1)), dma((ny, nx - 1)), dma((ny, NZ - 1)), dma((ny, NZ - 1)),
            dma((ny,)), dma((ny * NC,)), dma((NZ - 1,)), dma((NZ - 1,)),
            dma((NZ // NC, nx - 1)), dma((NZ // NC, nx - 1)), dma((4,)),
        ],
        compiler_params=pltpu.CompilerParams(
            collective_id=0, has_side_effects=True, vmem_limit_bytes=60 * 1024 * 1024
        ),
    )(tokens, cotangent, router_logits.T, routes.T, *weights)
    outs = outer_sums(resid, slot_x, slot_c)
    return (mixed, *(each[None] for each in outs))


def solution(mesh):
    ny = mesh.shape["expert"] // NC
    nx = mesh.shape["dp"] // NZ
    row = P("expert", None)
    mat = P("expert", "dp", None)
    return jax.shard_map(
        functools.partial(shards, nx, ny),
        mesh=mesh,
        in_specs=(row,) * 4 + (mat,) * 6,
        out_specs=(row, mat, mat, mat),
        check_vma=False,
    )
```

time: 154 us -> 67.3 us (0.44)
  Pallas kernels: 0 us -> 65.4 us
  waiting for transfers between devices: 50.7 us -> 0 us
  blocking collectives: 26 us -> 0 us
  starting transfers between devices: 25.2 us -> 0 us
  matrix products: 24.2 us -> 0 us
  local copies, waits for them, and re-layouts: 22.4 us -> 0.8 us
  other arithmetic: 3.12 us -> 0 us
    pallas_call x0 -> x2, Pallas kernels: none -> 65.4 us  [the longest x1 59.9 us: shards(): pl.pallas_call(functools.partial(layer_kernel, nx, ny, cap), out_shape=(s...]
    all_to_all x4 -> x0, waiting for transfers between devices: 50.7 us -> none  [the longest x1 28.3 us: summed_on_arrival(): lax.all_to_all(cut_along(value, dim, peers), axis, 0, 0, tiled=True)]
    all_to_all x1 -> x0, blocking collectives: 26 us -> none  [shards(): lax.all_to_all(send_rows, 'expert', split_axis=0, concat_axis=0, tiled=True)]
    all_to_all x4 -> x0, starting transfers between devices: 25.2 us -> none  [the longest x1 11.4 us: summed_on_arrival(): lax.all_to_all(cut_along(value, dim, peers), axis, 0, 0, tiled=True)]
    dot_general x13 -> x0, matrix products: 24.2 us -> none  [the longest x6 9.79 us: project(): jnp.einsum('rd,hd->rh', left_rows, matrix, preferred_element_type=jnp.flo...]
    convert_element_type x2 -> x0, local copies, waits for them, and re-layouts: 6.23 us -> none  [the longest x1 3.66 us: shards(): jnp.repeat(cotangent, top_count, axis=0).astype(jnp.float32)]
    broadcast_in_dim x3 -> x0, local copies, waits for them, and re-layouts: 6.04 us -> none  [the longest x1 3.45 us: shards(): jnp.repeat(cotangent, top_count, axis=0).astype(jnp.float32)]
    unnamed x20 -> x3, local copies, waits for them, and re-layouts: 6.61 us -> 0.8 us
  transfers between devices with their start and end apart: 4 -> 0, of which waited for: 4 -> 0; matrix products, arithmetic and copies ran while one was open for 22% -> 0% of each run, Pallas kernels for 0% -> 0%
where the time goes in v1:
time: 67.3 us; the launch traced here: 66.9 us
  Pallas kernels  65.4 us (97%)
  local copies, waits for them, and re-layouts  0.8 us (1%)
    pallas_call x1, Pallas kernels, shards(): pl.pallas_call(functools.partial(layer_kernel, nx, ny, cap), out_shape=(s...  59.9 us
    pallas_call x1, Pallas kernels, outer_sums(): pl.pallas_call(outer_kernel, grid=(width // step,), out_shape=(out, out,...  5.51 us

profile of v1, /device:TPU:32, one launch (start us, length us, event | category | flops | bytes accessed | tf_op | source)
XLA Modules:
  0.0 66.9 jit_solution(11413729559944666765)
XLA Ops:
  0.6 59.9 %shard_map.129 = (bf16[128,2048]{1,0:T(8,128)(2,1)}, bf16[384,2048]{1,0:T(8,128)(2,1)}, bf16[384,2048]{1,0:T(8,128)(2,1)}, bf16[3,224,384]{2,1,0:T(8,128)(2,1)}) custom-call(bf16[128,2048]{1,0:T(8,128)(2,1)} %refs_0_.1, bf16[128,2048]{1,0:T(8,128)(2,1)} %refs_1_.1, f32[2,128]{1,0:T(2,128)} %bitcast.17, s32[2,128]{1,0:T(2,128)} %bitcast.18, ...), custom_call_target="tpu_custom_call" | custom-call | tf_op jit(solution)/shard_map/pallas_call | solution.py:375
  60.6 0.0 copy-start
  60.6 5.5 %shard_map.130 = (f32[224,2048]{1,0:T(8,128)}, f32[224,2048]{1,0:T(8,128)}, f32[224,2048]{1,0:T(8,128)}) custom-call(bf16[3,224,384]{2,1,0:T(8,128)(2,1)} %get-tuple-element.12.resid, bf16[384,2048]{1,0:T(8,128)(2,1)} %get-tuple-element.13.slot_x, bf16[384,2048]{1,0:T(8,128)(2,1)} %get-tuple-element.14.slot_c), custom_call_target="tpu_custom_call" | custom-call | tf_op jit(solution)/shard_map/pallas_call | solution.py:349
  66.1 0.0 copy-done
  66.1 0.8 %copy.15 = bf16[128,2048]{1,0:T(8,128)(2,1)} copy(bf16[128,2048]{1,0:T(8,128)(2,1)S(1)} %copy-done) | data formatting | bytes 1048576
Async XLA Ops:
  60.6 5.5 %copy-start = (bf16[128,2048]{1,0:T(8,128)(2,1)S(1)}, bf16[128,2048]{1,0:T(8,128)(2,1)}, u32[]{:S(2)}) copy-start(bf16[128,2048]{1,0:T(8,128)(2,1)} %get-tuple-element.22) | copy-start | bytes 1572868

commit v2 on v1

--- a/solution.py
+++ b/solution.py
@@ -33,13 +33,13 @@
 
 def layer_kernel(nx, ny, cap, *refs):
     (
-        tok_hbm, cot_hbm, logits_ref, routes_ref, g_hbm, u_hbm, w_hbm, vg_hbm, vu_hbm, vw_hbm,
-        mixed_hbm, slotx_hbm, slotc_hbm, resid_hbm,
-        tok, cot, g, u, w, vg, vu, vw,
+        tok_hbm, cot_hbm, logits_hbm, routes_hbm, g_hbm, u_hbm, w_hbm, vg_hbm, vu_hbm, vw_hbm,
+        mixed, hvp_gate, hvp_up, hvp_down,
+        logits_ref, routes_ref, tok, cot, g, u, w, vg, vu, vw,
         disp, prob_t, send_x, send_c, slot_x, slot_c,
-        xsend, xrecv, xown, zsend, zrecv, ret_send, ret, mixed, resid,
+        xsend, xrecv, xown, zsend, zrecv, ret_send, ret,
         load_sem, tok_ss, tok_rs, cot_ss, cot_rs, x_ss, x_rs, z_ss, z_rs, r_ss, r_rs,
-        gz_ss, gz_rs, gx_ss, gx_rs, out_sem,
+        gz_ss, gz_rs, gx_ss, gx_rs,
     ) = refs
     tokens, width = tok.shape
     xw = width // nx
@@ -58,7 +58,7 @@
 
     loads = []
     for number, (src, dst) in enumerate(
-        [(tok_hbm, tok), (cot_hbm, cot), (g_hbm, g), (u_hbm, u), (w_hbm, w), (vg_hbm, vg), (vu_hbm, vu), (vw_hbm, vw)]
+        [(routes_hbm, routes_ref), (logits_hbm, logits_ref), (tok_hbm, tok), (cot_hbm, cot), (g_hbm, g), (u_hbm, u), (w_hbm, w), (vg_hbm, vg), (vu_hbm, vu), (vw_hbm, vw)]
     ):
         copy = pltpu.make_async_copy(src, dst, load_sem.at[number])
         copy.start()
@@ -76,6 +76,10 @@
                 peers.append(dict(dy=dy, dc=dc))
     for peer in peers:
         pl.semaphore_signal(barrier, inc=1, device_id=device(**peer), device_id_type=MESH)
+
+    loads[0].wait()
+    loads[1].wait()
+    loads = loads[2:]
 
     experts = ny * NC
     expert_iota = lax.broadcasted_iota(jnp.int32, (experts, tokens), 0)
@@ -96,8 +100,6 @@
     prob_t[0] = jnp.transpose(jnp.broadcast_to(first, (LANES, tokens)))
     prob_t[1] = 1.0 - prob_t[0]
 
-    pl.semaphore_wait(barrier, len(peers))
-
     sends = []
 
     def send(src, dst, ss, rs, target):
@@ -112,35 +114,36 @@
     order = [dy for dy in (1, ny - 1, 2) if dy < ny]
     order = [dy for i, dy in enumerate(order) if dy not in order[:i]] + [0]
 
-    def dispatch(buffer, target_buffer, ss, rs, values, hot):
+    def fill(buffer, own_buffer, values, hot):
+        for dy in order:
+            block = pl.ds(aligned((y + dy) % ny, pair), pair)
+            buffer[block, :] = dot_nn(hot(block), values).astype(BF16)
+        own_buffer[my_rows, :] = buffer[my_rows, :]
+
+    def dispatch(buffer, target_buffer, ss, rs):
         copies = {}
         for dy in order:
-            yy = (y + dy) % ny
-            block = pl.ds(aligned(yy, pair), pair)
-            buffer[block, :] = dot_nn(hot(block), values).astype(BF16)
             for dc in range(NC):
-                if dy == 0 and dc == 0:
-                    target_buffer[my_rows, :] = buffer[my_rows, :]
-                    continue
-                ee = yy * NC + (c + dc) % NC
-                number = dy * NC + dc
-                copies[number] = send(
-                    buffer.at[pl.ds(aligned(ee, cap), cap)], target_buffer.at[my_rows],
-                    ss.at[number], rs.at[number], device(dy=dy, dc=dc),
-                )
+                if dy or dc:
+                    ee = (y + dy) % ny * NC + (c + dc) % NC
+                    number = dy * NC + dc
+                    copies[number] = send(
+                        buffer.at[pl.ds(aligned(ee, cap), cap)], target_buffer.at[my_rows],
+                        ss.at[number], rs.at[number], device(dy=dy, dc=dc),
+                    )
         return copies
 
     loads[0].wait()
-    tok_copies = dispatch(
-        send_x, slot_x, tok_ss, tok_rs, tok[...],
-        lambda block: disp[block, :tokens] + disp[block, tokens:],
-    )
+    fill(send_x, slot_x, tok[...], lambda block: disp[block, :tokens] + disp[block, tokens:])
+    pl.semaphore_wait(barrier, len(peers))
+    tok_copies = dispatch(send_x, slot_x, tok_ss, tok_rs)
     loads[1].wait()
     cot_f = cot[...].astype(F32)
     scaled = jnp.concatenate(
         [(prob_t[0][:, 0:1] * cot_f).astype(BF16), (prob_t[1][:, 0:1] * cot_f).astype(BF16)], axis=0
     )
-    cot_copies = dispatch(send_c, slot_c, cot_ss, cot_rs, scaled, lambda block: disp[block, :])
+    fill(send_c, slot_c, scaled, lambda block: disp[block, :])
+    cot_copies = dispatch(send_c, slot_c, cot_ss, cot_rs)
 
     for copy in loads[2:5]:
         copy.wait()
@@ -227,8 +230,6 @@
     up = dot_nt(u[...], all_x)
     tang_gate = dot_nt(vg[...], all_x)
     tang_up = dot_nt(vu[...], all_x)
-    copy_x = pltpu.make_async_copy(slot_x, slotx_hbm, out_sem.at[0])
-    copy_x.start()
 
     reduce_z(groups[-2])
     reduce_z(groups[-1])
@@ -288,8 +289,6 @@
 
     for copy in cot_copies.values():
         copy.wait_recv()
-    copy_c = pltpu.make_async_copy(slot_c, slotc_hbm, out_sem.at[1])
-    copy_c.start()
     all_c = slot_c[...]
     back_grad = dot_nt(w[...], all_c)
     back_tang = dot_nt(vw[...], all_c)
@@ -298,18 +297,22 @@
     slope_one = sig * (1.0 + pre * (1.0 - sig))
     slope_two = sig * (1.0 - sig) * (2.0 + pre * (1.0 - 2.0 * sig))
     silu_tang = slope_one * tang_gate
-    resid[2] = (silu_tang * up + silu * tang_up).astype(BF16)
-    resid[0] = (
-        (back_tang * up + back_grad * tang_up) * slope_one + back_grad * up * slope_two * tang_gate
-    ).astype(BF16)
-    resid[1] = (back_tang * silu + back_grad * silu_tang).astype(BF16)
-    copy_r = pltpu.make_async_copy(resid, resid_hbm, out_sem.at[2])
-    copy_r.start()
+    def outer(left, right, target):
+        left = left.astype(BF16)
+        half = width // 2
+        for part in range(2):
+            columns = pl.ds(part * half, half)
+            target[:, columns] = dot_nn(left, right[:, columns])
+
+    outer(silu_tang * up + silu * tang_up, slot_c, hvp_down)
+    outer(back_tang * silu + back_grad * silu_tang, slot_x, hvp_up)
+    outer(
+        (back_tang * up + back_grad * tang_up) * slope_one + back_grad * up * slope_two * tang_gate,
+        slot_x, hvp_gate,
+    )
 
     for _, copy in x_gathers:
         copy.wait_recv()
-    copy_m = pltpu.make_async_copy(mixed, mixed_hbm, out_sem.at[3])
-    copy_m.start()
 
     for copy in sends:
         copy.wait_send()
@@ -327,36 +330,17 @@
         for dz in range(1, NZ):
             gather_z(dz).wait_send()
 
-    copy_x.wait()
-    copy_c.wait()
-    copy_r.wait()
-    copy_m.wait()
-
-
-def outer_kernel(resid, slot_x, slot_c, gate, up, down):
-    rows_x = slot_x[...]
-    gate[...] = dot_nn(resid[0], rows_x)
-    up[...] = dot_nn(resid[1], rows_x)
-    down[...] = dot_nn(resid[2], slot_c[...])
-
-
-def outer_sums(resid, slot_x, slot_c):
-    _, hidden, rows = resid.shape
-    width = slot_x.shape[1]
-    step = width // 4
-    out = jax.ShapeDtypeStruct((hidden, width), F32)
-    column = lambda i: (0, i)
-    return pl.pallas_call(
-        outer_kernel,
-        grid=(width // step,),
-        out_shape=(out, out, out),
-        in_specs=[
-            pl.BlockSpec((3, hidden, rows), lambda i: (0, 0, 0)),
-            pl.BlockSpec((rows, step), column),
-            pl.BlockSpec((rows, step), column),
-        ],
-        out_specs=[pl.BlockSpec((hidden, step), column)] * 3,
-    )(resid, slot_x, slot_c)
+
+def store_kernel(*refs):
+    *arrays, sems = refs
+    half = len(arrays) // 2
+    copies = [
+        pltpu.make_async_copy(arrays[i], arrays[half + i], sems.at[i]) for i in range(half)
+    ]
+    for copy in copies:
+        copy.start()
+    for copy in copies:
+        copy.wait()
 
 
 def shards(nx, ny, tokens, cotangent, router_logits, routes, *weights):
@@ -370,17 +354,20 @@
     dma = pltpu.SemaphoreType.DMA
     vmem = pltpu.VMEM
     any_spec = pl.BlockSpec(memory_space=pl.ANY)
+    hbm_spec = pl.BlockSpec(memory_space=pltpu.HBM)
     vmem_spec = pl.BlockSpec(memory_space=pltpu.VMEM)
     sds = jax.ShapeDtypeStruct
-    mixed, slot_x, slot_c, resid = pl.pallas_call(
+    hvp = sds((hidden, width), F32)
+    shapes = (sds((count, width), BF16), hvp, hvp, hvp)
+    args = (tokens, cotangent, router_logits.T, routes.T, *weights)
+    args = [pltpu.with_memory_space_constraint(each, pltpu.HBM) for each in args]
+    results = pl.pallas_call(
         functools.partial(layer_kernel, nx, ny, cap),
-        out_shape=(
-            sds((count, width), BF16), sds((rows, width), BF16), sds((rows, width), BF16),
-            sds((3, hidden, rows), BF16),
-        ),
-        in_specs=[any_spec, any_spec, vmem_spec, vmem_spec] + [any_spec] * 6,
-        out_specs=[any_spec] * 4,
-        scratch_shapes=[vmem((count, width), BF16)] * 2
+        out_shape=tuple(pltpu.VMEM(each.shape, each.dtype) for each in shapes),
+        in_specs=[hbm_spec] * 10,
+        out_specs=[vmem_spec] * 4,
+        scratch_shapes=[vmem(args[2].shape, F32), vmem(args[3].shape, jnp.int32)]
+        + [vmem((count, width), BF16)] * 2
         + [vmem((hidden, width), BF16)] * 6
         + [vmem((rows, 2 * count), BF16), vmem((2, count, LANES), F32)]
         + [vmem((rows, width), BF16)] * 4
@@ -388,17 +375,24 @@
             vmem((ny, nx - 1, pair, xw), BF16), vmem((ny, nx - 1, pair, xw), BF16),
             vmem((ny, pair, xw), F32), vmem((ny, pair, xw), BF16),
             vmem((ny, NZ - 1, cap, LANES), BF16), vmem((ny, cap, LANES), BF16),
-            vmem((rows, LANES), BF16), vmem((count, width), BF16), vmem((3, hidden, rows), BF16),
-            dma((8,)), dma((ny * NC,)), dma((ny * NC,)), dma((ny * NC,)), dma((ny * NC,)),
+            vmem((rows, LANES), BF16),
+            dma((10,)), dma((ny * NC,)), dma((ny * NC,)), dma((ny * NC,)), dma((ny * NC,)),
             dma((ny, nx - 1)), dma((ny, nx - 1)), dma((ny, NZ - 1)), dma((ny, NZ - 1)),
             dma((ny,)), dma((ny * NC,)), dma((NZ - 1,)), dma((NZ - 1,)),
-            dma((NZ // NC, nx - 1)), dma((NZ // NC, nx - 1)), dma((4,)),
+            dma((NZ // NC, nx - 1)), dma((NZ // NC, nx - 1)),
         ],
         compiler_params=pltpu.CompilerParams(
-            collective_id=0, has_side_effects=True, vmem_limit_bytes=60 * 1024 * 1024
+            collective_id=0, has_side_effects=True, vmem_limit_bytes=36 * 1024 * 1024
         ),
-    )(tokens, cotangent, router_logits.T, routes.T, *weights)
-    outs = outer_sums(resid, slot_x, slot_c)
+    )(*args)
+    mixed, *outs = pl.pallas_call(
+        store_kernel,
+        out_shape=tuple(pltpu.HBM(each.shape, each.dtype) for each in shapes),
+        in_specs=[any_spec] * 4,
+        out_specs=[hbm_spec] * 4,
+        scratch_shapes=[dma((4,))],
+        compiler_params=pltpu.CompilerParams(vmem_limit_bytes=1024 * 1024),
+    )(*[pltpu.with_memory_space_constraint(each, pltpu.VMEM) for each in results])
     return (mixed, *(each[None] for each in outs))
 
 

time: 67.3 us -> 61.9 us (0.920)
  Pallas kernels: 65.4 us -> 61.2 us
  local copies, waits for them, and re-layouts: 0.8 us -> 0 us
    pallas_call x2, Pallas kernels: 65.4 us -> 61.2 us  [the longest x1 58.5 us: shards(): pl.pallas_call(functools.partial(layer_kernel, nx, ny, cap), out_shape=tu...]
    unnamed x3 -> x0, local copies, waits for them, and re-layouts: 0.8 us -> none
where the time goes in v2:
time: 61.9 us; the launch traced here: 61.8 us
  Pallas kernels  61.2 us (99%)
  between operations  0.64 us (1%)
    pallas_call x1, Pallas kernels, shards(): pl.pallas_call(functools.partial(layer_kernel, nx, ny, cap), out_shape=tu...  58.5 us
    pallas_call x1, Pallas kernels, shards(): pl.pallas_call(store_kernel, out_shape=tuple((pltpu.HBM(each.shape, each....  2.65 us

profile of v2, /device:TPU:32, one launch (start us, length us, event | category | flops | bytes accessed | tf_op | source)
XLA Modules:
  0.0 61.8 jit_solution(17647845926269714240)
XLA Ops:
  0.6 58.5 %shard_map.129 = (bf16[128,2048]{1,0:T(8,128)(2,1)S(1)}, f32[224,2048]{1,0:T(8,128)S(1)}, f32[224,2048]{1,0:T(8,128)S(1)}, f32[224,2048]{1,0:T(8,128)S(1)}) custom-call(bf16[128,2048]{1,0:T(8,128)(2,1)} %refs_0_.1, bf16[128,2048]{1,0:T(8,128)(2,1)} %refs_1_.1, f32[2,128]{1,0:T(2,128)} %bitcast.17, s32[2,128]{1,0:T(2,128)} %bitcast.18, ...), custom_call_target="tpu_custom_call" | custom-call | tf_op jit(solution)/shard_map/pallas_call | solution.py:364
  59.2 2.6 %shard_map.130 = (bf16[128,2048]{1,0:T(8,128)(2,1)}, f32[224,2048]{1,0:T(8,128)}, f32[224,2048]{1,0:T(8,128)}, f32[224,2048]{1,0:T(8,128)}) custom-call(bf16[128,2048]{1,0:T(8,128)(2,1)S(1)} %get-tuple-element.12.refs_0_, f32[224,2048]{1,0:T(8,128)S(1)} %get-tuple-element.13.refs_1_, f32[224,2048]{1,0:T(8,128)S(1)} %get-tuple-element.14.refs_2_, ...), custom_call_target="tpu_custom_call" | custom-call | tf_op jit(solution)/shard_map/pallas_call | solution.py:388

commit v3 on v2

v3 whole, which is shorter than its diff:
```python
import functools

import jax
import jax.numpy as jnp
from jax import lax
from jax.experimental import pallas as pl
from jax.experimental.pallas import tpu as pltpu
from jax.sharding import PartitionSpec as P

MESH = pl.DeviceIdType.MESH
F32 = jnp.float32
BF16 = jnp.bfloat16
NZ = 8
NC = 2
LANES = 128


def dot_nt(left, right):
    return lax.dot_general(left, right, (((1,), (1,)), ((), ())), preferred_element_type=F32)


def dot_tn(left, right):
    return lax.dot_general(left, right, (((0,), (0,)), ((), ())), preferred_element_type=F32)


def dot_nn(left, right):
    return jnp.dot(left, right, preferred_element_type=F32)


def aligned(index, size):
    return pl.multiple_of(index * size, size)


def layer_kernel(nx, ny, cap, *refs):
    (
        tok_hbm, cot_hbm, logits_hbm, routes_hbm, g_hbm, u_hbm, w_hbm, vg_hbm, vu_hbm, vw_hbm,
        mixed, hvp_gate, hvp_up, hvp_down,
        logits_ref, routes_ref, tok, cot, g, u, w, vg, vu, vw,
        disp, prob_t, send_x, send_c, slot_x, slot_c,
        xsend, xrecv, xown, zsend, final,
        load_sem, send_sem, tok_rs, x_rs, one_rs, gz_rs,
    ) = refs
    tokens, width = tok.shape
    xw = width // nx
    pair = NC * cap
    rows = ny * pair

    dp = lax.axis_index("dp")
    e = lax.axis_index("expert")
    x, z = dp // NZ, dp % NZ
    y, c = e // NC, e % NC
    parity = z % NC
    away = (c + parity) % NC

    def device(dx=0, dz=0, dy=0, dc=0):
        return (((x + dx) % nx) * NZ + (z + dz) % NZ, ((y + dy) % ny) * NC + (c + dc) % NC)

    loads = []
    for number, (src, dst) in enumerate(
        [(routes_hbm, routes_ref), (logits_hbm, logits_ref), (tok_hbm, tok), (cot_hbm, cot), (g_hbm, g), (u_hbm, u), (w_hbm, w), (vg_hbm, vg), (vu_hbm, vu), (vw_hbm, vw)]
    ):
        copy = pltpu.make_async_copy(src, dst, load_sem.at[number])
        copy.start()
        loads.append(copy)

    barrier = pltpu.get_barrier_semaphore()
    peers = []
    for dx in range(1, nx):
        peers.append(dict(dx=dx))
    for dz in range(1, NZ):
        peers.append(dict(dz=dz))
    for dy in range(ny):
        for dc in range(NC):
            if dy or dc:
                peers.append(dict(dy=dy, dc=dc))
    for peer in peers:
        pl.semaphore_signal(barrier, inc=1, device_id=device(**peer), device_id_type=MESH)

    loads[0].wait()
    loads[1].wait()
    loads = loads[2:]

    experts = ny * NC
    expert_iota = lax.broadcasted_iota(jnp.int32, (experts, tokens), 0)
    route0, route1 = routes_ref[0:1, :], routes_ref[1:2, :]
    hot0 = (expert_iota == route0).astype(F32)
    hot1 = (expert_iota == route1).astype(F32)
    before = (
        lax.broadcasted_iota(jnp.int32, (tokens, tokens), 0)
        < lax.broadcasted_iota(jnp.int32, (tokens, tokens), 1)
    ).astype(BF16)
    earlier = dot_nn((hot0 + hot1).astype(BF16), before)
    pos0 = jnp.sum(earlier * hot0, axis=0, keepdims=True).astype(jnp.int32)
    pos1 = jnp.sum(earlier * hot1, axis=0, keepdims=True).astype(jnp.int32)
    slot_iota = lax.broadcasted_iota(jnp.int32, (rows, tokens), 0)
    disp[:, :tokens] = (slot_iota == route0 * cap + pos0).astype(F32).astype(BF16)
    disp[:, tokens:] = (slot_iota == route1 * cap + pos1).astype(F32).astype(BF16)
    first = jax.nn.sigmoid(logits_ref[0:1, :] - logits_ref[1:2, :])
    prob_t[0] = jnp.transpose(jnp.broadcast_to(first, (LANES, tokens)))
    prob_t[1] = 1.0 - prob_t[0]

    cot_rs, far_rs, fin_rs, gx_rs = (one_rs.at[number] for number in range(4))
    tok_ss, cot_ss, x_ss, fin_ss, far_ss, own_ss, gz_ss, gx_ss, tokf_ss = (
        send_sem.at[number] for number in range(9)
    )

    def remote(src, dst, ss, rs, target):
        return pltpu.make_async_remote_copy(
            src_ref=src, dst_ref=dst, send_sem=ss, recv_sem=rs, device_id=target, device_id_type=MESH
        )

    def send(*args):
        remote(*args).start()

    def sent(ref, ss):
        remote(ref, ref, ss, gx_rs, (dp, e)).wait_send()

    def received(ref, rs):
        remote(ref, ref, gx_ss, rs, (dp, e)).wait_recv()

    my_rows = pl.ds(aligned(e, cap), cap)
    order = [dy for dy in (1, ny - 1, 2) if dy < ny]
    order = [dy for i, dy in enumerate(order) if dy not in order[:i]] + [0]

    def fill(buffer, own_buffer, values, hot):
        for dy in order:
            block = pl.ds(aligned((y + dy) % ny, pair), pair)
            buffer[block, :] = dot_nn(hot(block), values).astype(BF16)
        own_buffer[my_rows, :] = buffer[my_rows, :]

    far = ny // 2 if ny > 2 else 0
    share = width // NZ
    my_share = pl.ds(aligned(z, share), share)

    def arrival(dy, dc):
        return 0 if dy == far and far else 1 if dy == 0 else 2 + dc

    def dispatch(buffer, target_buffer, through_z, blocks):
        for dy, dc in blocks:
            ee = (y + dy) % ny * NC + (c + dc) % NC
            part = through_z and dy == far and far
            columns = my_share if part else pl.ds(0, width)
            send(
                buffer.at[pl.ds(aligned(ee, cap), cap), columns], target_buffer.at[my_rows, columns],
                (tokf_ss if part else tok_ss) if through_z else cot_ss,
                tok_rs.at[arrival(dy, dc)] if through_z else cot_rs, device(dy=dy, dc=dc),
            )

    near = [dy for dy in order if dy and dy != far]
    direct_order = [(0, 1)] + [(dy, dc) for dy in near + [far] if dy for dc in range(NC)]
    through_order = [(far, dc) for dc in range(NC)] if far else []
    through_order += [(0, 1)] + [(dy, dc) for dc in range(NC) for dy in near]

    loads[0].wait()
    fill(send_x, slot_x, tok[...], lambda block: disp[block, :tokens] + disp[block, tokens:])
    pl.semaphore_wait(barrier, len(peers))
    dispatch(send_x, slot_x, True, through_order)
    loads[1].wait()
    cot_f = cot[...].astype(F32)
    scaled = jnp.concatenate(
        [(prob_t[0][:, 0:1] * cot_f).astype(BF16), (prob_t[1][:, 0:1] * cot_f).astype(BF16)], axis=0
    )
    fill(send_c, slot_c, scaled, lambda block: disp[block, :])
    dispatch(send_c, slot_c, False, direct_order[:-2] if far else direct_order)

    for copy in loads[2:5]:
        copy.wait()

    z_order = [dz for dz in (4, 3, 5, 2, 6, 1, 7) if dz < NZ]

    def group_rows(dy):
        return pl.ds(aligned((y - dy) % ny, pair), pair)

    def forward(blocks):
        together = len({dy for dy, _ in blocks}) == 1
        if together:
            rows_x = slot_x[group_rows(blocks[0][0]), :]
        else:
            rows_x = jnp.concatenate(
                [slot_x[pl.ds(aligned((y - dy) % ny * NC + (c + dc) % NC, cap), cap), :] for dy, dc in blocks],
                axis=0,
            )
        pre = dot_nt(rows_x, g[...])
        up = dot_nt(rows_x, u[...])
        hidden = (pre * jax.nn.sigmoid(pre) * up).astype(BF16)
        for dx in list(range(1, nx)) + [0]:
            xx = (x + dx) % nx
            part = dot_nn(hidden, w[:, pl.ds(aligned(xx, xw), xw)])
            for number, (dy, dc) in enumerate([(blocks[0][0], 0)] if together else blocks):
                place = pl.ds(0, pair) if together else pl.ds(aligned((c + dc) % NC, cap), cap)
                value = part if together else part[number * cap : (number + 1) * cap]
                if dx == 0:
                    xown[dy, place] = value
                else:
                    xsend[dy, dx - 1, place] = value.astype(BF16)
                    send(
                        xsend.at[dy, dx - 1, place], xrecv.at[dy, dx - 1, place],
                        x_ss, x_rs.at[dy], device(dx=dx),
                    )

    def spread_far():
        received(slot_x.at[pl.ds(0, pair), pl.ds(0, share)], tok_rs.at[0])
        part = slot_x.at[group_rows(far), my_share]
        for dz in z_order:
            send(part, part, far_ss, far_rs, device(dz=dz))

    def reduce_x(dy):
        received(xrecv.at[dy], x_rs.at[dy])
        total = xown[dy]
        for dx in range(1, nx):
            total = total + xrecv[dy, dx - 1].astype(F32)
        zsend[dy] = total.astype(BF16)
        for dz in z_order:
            final_copy(dy, dz).start()
        if dy:
            final_copy(dy, 0).start()
        else:
            @pl.when(away == 1)
            def _():
                final_copy(0, 0).start()

            @pl.when(away == 0)
            def _():
                final[my_final, :] = zsend.at[final_part(0, z)][...]

    my_final = pl.ds(aligned(z * experts + e, cap), cap)

    def final_part(dy, zz):
        return (dy, pl.ds(aligned(zz % NC, cap), cap), pl.ds(aligned(zz // NC, LANES), LANES))

    def final_copy(dy, dz):
        zz = (z + dz) % NZ
        target = (x * NZ + zz, (y - dy + ny) % ny * NC + zz % NC)
        return remote(
            zsend.at[final_part(dy, zz)], final.at[my_final], fin_ss if dy or dz else own_ss, fin_rs, target
        )

    received(slot_x.at[pl.ds(0, cap)], tok_rs.at[1])
    forward([(0, 0), (0, 1)])
    if far:
        spread_far()
    for dc in range(NC):
        received(slot_x.at[pl.ds(0, cap * len(near))], tok_rs.at[2 + dc])
        forward([(dy, dc) for dy in near])
        if dc == 0:
            reduce_x(0)
        elif far:
            dispatch(send_c, slot_c, False, direct_order[-2:-1])
    if far:
        received(slot_x.at[pl.ds(0, pair), pl.ds(0, width - share)], far_rs)
        forward([(far, 0), (far, 1)])
    for dy in near:
        reduce_x(dy)

    for copy in loads[5:8]:
        copy.wait()
    all_x = slot_x[...]
    pre = dot_nt(g[...], all_x)
    up = dot_nt(u[...], all_x)
    tang_gate = dot_nt(vg[...], all_x)
    tang_up = dot_nt(vu[...], all_x)

    if far:
        reduce_x(far)
        dispatch(send_c, slot_c, False, direct_order[-1:])

    def piece(xx, zz):
        return mixed.at[:, pl.ds(aligned(xx * (xw // LANES) + zz // NC, LANES), LANES)]

    def gather_z(dz):
        return pltpu.make_async_remote_copy(
            src_ref=piece(x, z), dst_ref=piece(x, z), send_sem=gz_ss,
            recv_sem=gz_rs.at[dz - 1], device_id=device(dz=dz), device_id_type=MESH,
        )

    @pl.when(away == 0)
    def _():
        received(final.at[pl.ds(0, NZ * rows - cap)], fin_rs)
        total = final[pl.ds(0, rows), :].astype(F32)
        for zz in range(1, NZ):
            total = total + final[pl.ds(zz * rows, rows), :].astype(F32)
        returned = total.astype(BF16)
        picked0 = dot_tn(disp[:, :tokens], returned)
        picked1 = dot_tn(disp[:, tokens:], returned)
        piece(x, z)[...] = (prob_t[0] * picked0 + prob_t[1] * picked1).astype(BF16)
        for dz in range(1, NZ):
            gather_z(dz).start()

    def pass_on(number, source=None):
        back = NC * number + (away if source is None else 1 - source)
        zz = (z + NZ - back) % NZ
        part = piece(x, zz)
        if number or not source:
            received(part, gz_rs.at[back - 1])
        for dx in range(1, nx):
            send(part, part, gx_ss, gx_rs, device(dx=dx))

    @pl.when(away == 0)
    def _():
        pass_on(0, True)

    def outer(left, right, target):
        left = left.astype(BF16)
        half = width // 2
        for part in range(2):
            columns = pl.ds(part * half, half)
            target[:, columns] = dot_nn(left, right[:, columns])

    @pl.when(away == 1)
    def _():
        pass_on(0, False)

    for number in (3, 1, 2):
        if number < NZ // NC:
            pass_on(number)

    received(slot_c.at[pl.ds(0, rows - cap)], cot_rs)
    all_c = slot_c[...]
    back_grad = dot_nt(w[...], all_c)
    back_tang = dot_nt(vw[...], all_c)
    sig = jax.nn.sigmoid(pre)
    silu = pre * sig
    slope_one = sig * (1.0 + pre * (1.0 - sig))
    slope_two = sig * (1.0 - sig) * (2.0 + pre * (1.0 - 2.0 * sig))
    silu_tang = slope_one * tang_gate
    outer(silu_tang * up + silu * tang_up, slot_c, hvp_down)
    outer(back_tang * silu + back_grad * silu_tang, slot_x, hvp_up)
    outer(
        (back_tang * up + back_grad * tang_up) * slope_one + back_grad * up * slope_two * tang_gate,
        slot_x, hvp_gate,
    )

    gathered = NZ // NC * (nx - 1) * LANES
    received(mixed.at[:, pl.ds(0, gathered)], gx_rs)

    direct = 1 + NC * len(near)
    sent(slot_x.at[pl.ds(0, direct * cap)], tok_ss)
    sent(slot_c.at[pl.ds(0, rows - cap)], cot_ss)
    if far:
        sent(slot_x.at[pl.ds(0, pair), pl.ds(0, share)], tokf_ss)
        sent(slot_x.at[pl.ds(0, pair), pl.ds(0, width - share)], far_ss)
    sent(xsend, x_ss)
    sent(final.at[pl.ds(0, (ny * NZ - 1) * cap)], fin_ss)
    sent(mixed.at[:, pl.ds(0, gathered)], gx_ss)

    @pl.when(away == 1)
    def _():
        sent(final.at[pl.ds(0, cap)], own_ss)

    @pl.when(away == 0)
    def _():
        sent(mixed.at[:, pl.ds(0, (NZ - 1) * LANES)], gz_ss)


def store_kernel(*refs):
    *arrays, sems = refs
    half = len(arrays) // 2
    copies = [
        pltpu.make_async_copy(arrays[i], arrays[half + i], sems.at[i]) for i in range(half)
    ]
    for copy in copies:
        copy.start()
    for copy in copies:
        copy.wait()


def shards(nx, ny, tokens, cotangent, router_logits, routes, *weights):
    count, width = tokens.shape
    hidden = weights[0].shape[1]
    cap = routes.shape[1] * count * 3 // (2 * ny * NC)
    pair = NC * cap
    rows = ny * pair
    xw = width // nx
    weights = [each.reshape(hidden, width) for each in weights]
    dma = pltpu.SemaphoreType.DMA
    vmem = pltpu.VMEM
    any_spec = pl.BlockSpec(memory_space=pl.ANY)
    hbm_spec = pl.BlockSpec(memory_space=pltpu.HBM)
    vmem_spec = pl.BlockSpec(memory_space=pltpu.VMEM)
    sds = jax.ShapeDtypeStruct
    hvp = sds((hidden, width), F32)
    shapes = (sds((count, width), BF16), hvp, hvp, hvp)
    args = (tokens, cotangent, router_logits.T, routes.T, *weights)
    args = [pltpu.with_memory_space_constraint(each, pltpu.HBM) for each in args]
    results = pl.pallas_call(
        functools.partial(layer_kernel, nx, ny, cap),
        out_shape=tuple(pltpu.VMEM(each.shape, each.dtype) for each in shapes),
        in_specs=[hbm_spec] * 10,
        out_specs=[vmem_spec] * 4,
        scratch_shapes=[vmem(args[2].shape, F32), vmem(args[3].shape, jnp.int32)]
        + [vmem((count, width), BF16)] * 2
        + [vmem((hidden, width), BF16)] * 6
        + [vmem((rows, 2 * count), BF16), vmem((2, count, LANES), F32)]
        + [vmem((rows, width), BF16)] * 4
        + [
            vmem((ny, nx - 1, pair, xw), BF16), vmem((ny, nx - 1, pair, xw), BF16),
            vmem((ny, pair, xw), F32), vmem((ny, pair, xw), BF16),
            vmem((NZ * rows, LANES), BF16),
            dma((10,)), dma((9,)), dma((2 + NC,)), dma((ny,)), dma((4,)), dma((NZ - 1,)),
        ],
        compiler_params=pltpu.CompilerParams(
            collective_id=0, has_side_effects=True, vmem_limit_bytes=36 * 1024 * 1024
        ),
    )(*args)
    mixed, *outs = pl.pallas_call(
        store_kernel,
        out_shape=tuple(pltpu.HBM(each.shape, each.dtype) for each in shapes),
        in_specs=[any_spec] * 4,
        out_specs=[hbm_spec] * 4,
        scratch_shapes=[dma((4,))],
        compiler_params=pltpu.CompilerParams(vmem_limit_bytes=1024 * 1024),
    )(*[pltpu.with_memory_space_constraint(each, pltpu.VMEM) for each in results])
    return (mixed, *(each[None] for each in outs))


def solution(mesh):
    ny = mesh.shape["expert"] // NC
    nx = mesh.shape["dp"] // NZ
    row = P("expert", None)
    mat = P("expert", "dp", None)
    return jax.shard_map(
        functools.partial(shards, nx, ny),
        mesh=mesh,
        in_specs=(row,) * 4 + (mat,) * 6,
        out_specs=(row, mat, mat, mat),
        check_vma=False,
    )
```

time: 61.9 us -> 55.1 us (0.89)
  Pallas kernels: 61.2 us -> 53.8 us
    pallas_call x1, Pallas kernels: 58.5 us -> 51.1 us  [shards(): pl.pallas_call(functools.partial(layer_kernel, nx, ny, cap), out_shape=tu...]
where the time goes in v3:
time: 55.1 us; the launch traced here: 54.4 us
  Pallas kernels  53.8 us (98%)
  between operations  0.64 us (1%)
    pallas_call x1, Pallas kernels, shards(): pl.pallas_call(functools.partial(layer_kernel, nx, ny, cap), out_shape=tu...  51.1 us
    pallas_call x1, Pallas kernels, shards(): pl.pallas_call(store_kernel, out_shape=tuple((pltpu.HBM(each.shape, each....  2.65 us

profile of v3, /device:TPU:32, one launch (start us, length us, event | category | flops | bytes accessed | tf_op | source)
XLA Modules:
  0.0 54.4 jit_solution(8728963507522459844)
XLA Ops:
  0.6 51.1 %shard_map.129 = (bf16[128,2048]{1,0:T(8,128)(2,1)S(1)}, f32[224,2048]{1,0:T(8,128)S(1)}, f32[224,2048]{1,0:T(8,128)S(1)}, f32[224,2048]{1,0:T(8,128)S(1)}) custom-call(bf16[128,2048]{1,0:T(8,128)(2,1)} %refs_0_.1, bf16[128,2048]{1,0:T(8,128)(2,1)} %refs_1_.1, f32[2,128]{1,0:T(2,128)} %bitcast.17, s32[2,128]{1,0:T(2,128)} %bitcast.18, ...), custom_call_target="tpu_custom_call" | custom-call | tf_op jit(solution)/shard_map/pallas_call | solution.py:385
  51.8 2.6 %shard_map.130 = (bf16[128,2048]{1,0:T(8,128)(2,1)}, f32[224,2048]{1,0:T(8,128)}, f32[224,2048]{1,0:T(8,128)}, f32[224,2048]{1,0:T(8,128)}) custom-call(bf16[128,2048]{1,0:T(8,128)(2,1)S(1)} %get-tuple-element.12.refs_0_, f32[224,2048]{1,0:T(8,128)S(1)} %get-tuple-element.13.refs_1_, f32[224,2048]{1,0:T(8,128)S(1)} %get-tuple-element.14.refs_2_, ...), custom_call_target="tpu_custom_call" | custom-call | tf_op jit(solution)/shard_map/pallas_call | solution.py:405

commit v4 on v3

--- a/solution.py
+++ b/solution.py
@@ -259,6 +259,12 @@
     up = dot_nt(u[...], all_x)
     tang_gate = dot_nt(vg[...], all_x)
     tang_up = dot_nt(vu[...], all_x)
+    sig = jax.nn.sigmoid(pre)
+    silu = pre * sig
+    slope_one = sig * (1.0 + pre * (1.0 - sig))
+    slope_two = sig * (1.0 - sig) * (2.0 + pre * (1.0 - 2.0 * sig))
+    silu_tang = slope_one * tang_gate
+    hidden_tang = (silu_tang * up + silu * tang_up).astype(BF16)
 
     if far:
         reduce_x(far)
@@ -318,12 +324,7 @@
     all_c = slot_c[...]
     back_grad = dot_nt(w[...], all_c)
     back_tang = dot_nt(vw[...], all_c)
-    sig = jax.nn.sigmoid(pre)
-    silu = pre * sig
-    slope_one = sig * (1.0 + pre * (1.0 - sig))
-    slope_two = sig * (1.0 - sig) * (2.0 + pre * (1.0 - 2.0 * sig))
-    silu_tang = slope_one * tang_gate
-    outer(silu_tang * up + silu * tang_up, slot_c, hvp_down)
+    outer(hidden_tang, slot_c, hvp_down)
     outer(back_tang * silu + back_grad * silu_tang, slot_x, hvp_up)
     outer(
         (back_tang * up + back_grad * tang_up) * slope_one + back_grad * up * slope_two * tang_gate,

time: 55.1 us -> 55.1 us (level)
  no operation moved by 1% of the time
where the time goes in v4:
time: 55.1 us; the launch traced here: 54.4 us
  Pallas kernels  53.8 us (98%)
  between operations  0.64 us (1%)
    pallas_call x1, Pallas kernels, shards(): pl.pallas_call(functools.partial(layer_kernel, nx, ny, cap), out_shape=tu...  51.1 us
    pallas_call x1, Pallas kernels, shards(): pl.pallas_call(store_kernel, out_shape=tuple((pltpu.HBM(each.shape, each....  2.65 us

profile of v4, /device:TPU:32, one launch (start us, length us, event | category | flops | bytes accessed | tf_op | source)
XLA Modules:
  0.0 54.4 jit_solution(6302610535524380256)
XLA Ops:
  0.6 51.1 %shard_map.129 = (bf16[128,2048]{1,0:T(8,128)(2,1)S(1)}, f32[224,2048]{1,0:T(8,128)S(1)}, f32[224,2048]{1,0:T(8,128)S(1)}, f32[224,2048]{1,0:T(8,128)S(1)}) custom-call(bf16[128,2048]{1,0:T(8,128)(2,1)} %refs_0_.1, bf16[128,2048]{1,0:T(8,128)(2,1)} %refs_1_.1, f32[2,128]{1,0:T(2,128)} %bitcast.17, s32[2,128]{1,0:T(2,128)} %bitcast.18, ...), custom_call_target="tpu_custom_call" | custom-call | tf_op jit(solution)/shard_map/pallas_call | solution.py:386
  51.8 2.6 %shard_map.130 = (bf16[128,2048]{1,0:T(8,128)(2,1)}, f32[224,2048]{1,0:T(8,128)}, f32[224,2048]{1,0:T(8,128)}, f32[224,2048]{1,0:T(8,128)}) custom-call(bf16[128,2048]{1,0:T(8,128)(2,1)S(1)} %get-tuple-element.12.refs_0_, f32[224,2048]{1,0:T(8,128)S(1)} %get-tuple-element.13.refs_1_, f32[224,2048]{1,0:T(8,128)S(1)} %get-tuple-element.14.refs_2_, ...), custom_call_target="tpu_custom_call" | custom-call | tf_op jit(solution)/shard_map/pallas_call | solution.py:406
